TPU v7x, 32 devices: a whole 2x2x4 slice. The times are simulated.
32 devices in a mesh: pix: 8 (over z, y), rep: 4 (over x, core).
Axes of the slice: x: 2, y: 2, z: 4, core: 2. Of those that a mesh axis runs over, the one named last changes fastest.
Arguments:
- interferograms: float32 [256, 131072], P(('pix', 'rep')), may hold values from -6 to 6
- epoch_pairs: int32 [2, 256], replicated, may hold values from 0 to 63, as said below
- los: float32 [3, 131072], P(None, ('pix', 'rep')), may hold values from 0.3 to 1
- patch_place: int32 [2, 4096], replicated, may hold values from 0 to 255, as said below
- patch_depth: int32 [4096], replicated, may hold values from 0 to 7
Outputs:
- predicted: float32 [64, 131072], P(None, ('pix', 'rep'))
- slip: float32 [64, 4096], P(None, ('pix', 'rep'))
Inputs may be any that keep to these rules, and one draw needn't show every extreme that they name: `epoch_pairs`: row 0 holds an interferogram's earlier epoch and row 1 its later one; the two always differ. `patch_place`: row 0 is an east cell below 256; row 1 is a north cell below 32.
All inputs are finite; a program needn't handle non-finite values.
Results may differ from a plain program's by a relative error of at most 0.0037.
Values may be sent and summed in bfloat16 or wider, within the bound.
A program may use at most 64 MiB of HBM per device.

v0:
```python
import jax
import jax.numpy as jnp
from jax import lax
from jax.sharding import PartitionSpec as P

NEP = 64
IMG_W = 1024
pixel_step = 0.1
patch_step = 0.4
damping = 0.5
depth_base = 0.5
depth_step = 0.25


def sbas_inverse(epoch_pairs, epochs_count):
    epochs = lax.iota(jnp.int32, epochs_count)
    design = (epochs[None, :] == epoch_pairs[1][:, None]).astype(jnp.float32) - (
        epochs[None, :] == epoch_pairs[0][:, None]
    ).astype(jnp.float32)
    normal = jnp.dot(design.T, design, precision=lax.Precision.HIGHEST) + damping * jnp.eye(
        epochs_count, dtype=jnp.float32
    )
    factor = jnp.linalg.cholesky(normal)
    return jax.scipy.linalg.cho_solve((factor, True), design.T)


def green_tile(pixel, los_rows, patch_place, patch_depth):
    column = (pixel % IMG_W).astype(jnp.float32)
    line = (pixel // IMG_W).astype(jnp.float32)
    xpos = (column + 0.5) * pixel_step
    ypos = (line + 0.5) * pixel_step
    patch_x = (patch_place[0].astype(jnp.float32) + 0.5) * patch_step
    patch_y = (patch_place[1].astype(jnp.float32) + 0.5) * patch_step
    patch_z = depth_base + depth_step * patch_depth.astype(jnp.float32)
    delta_x = xpos[:, None] - patch_x[None, :]
    delta_y = ypos[:, None] - patch_y[None, :]
    delta_z = patch_z[None, :]
    dist_sq = delta_x * delta_x + delta_y * delta_y + delta_z * delta_z
    toward = (
        los_rows[0][:, None] * delta_x
        + los_rows[1][:, None] * delta_y
        + los_rows[2][:, None] * delta_z
    )
    return (delta_z * toward / (dist_sq * jnp.sqrt(dist_sq))).astype(jnp.bfloat16)


def on_device(interferograms, epoch_pairs, los, patch_place, patch_depth):
    devices = lax.axis_size(("pix", "rep"))
    ifg_dev, total = interferograms.shape
    pix_dev = total // devices
    epochs_count = NEP
    npatch = patch_depth.shape[0]
    own = npatch // devices
    pseudo = sbas_inverse(epoch_pairs, epochs_count)
    pieces = interferograms.reshape(ifg_dev, devices, pix_dev)
    series = jnp.dot(
        pseudo,
        lax.all_to_all(pieces, ("pix", "rep"), split_axis=1, concat_axis=0, tiled=True)[:, 0, :],
        precision=lax.Precision.HIGHEST,
        preferred_element_type=jnp.float32,
    )
    anchor = lax.axis_index(("pix", "rep")) * pix_dev
    width = min(512, pix_dev)
    count = pix_dev // width

    def tile_at(index):
        start = index * width
        pixel = anchor + start + lax.iota(jnp.int32, width)
        los_rows = lax.dynamic_slice_in_dim(los, start, width, 1)
        return (green_tile(pixel, los_rows, patch_place, patch_depth), start)

    def first_step(index, carry):
        rhs, bound = carry
        tile, start = tile_at(index)
        resid = lax.dynamic_slice_in_dim(series, start, width, 1).astype(jnp.bfloat16)
        rhs = rhs + jnp.dot(resid, tile, preferred_element_type=jnp.float32)
        magnitude = jnp.abs(tile)
        weight = jnp.sum(magnitude.astype(jnp.float32), axis=1).astype(jnp.bfloat16)
        bound = bound + jnp.dot(weight[None, :], magnitude, preferred_element_type=jnp.float32)
        return (rhs, bound)

    zero_rhs = jnp.zeros((epochs_count, npatch), jnp.float32)
    zero_bound = jnp.zeros((1, npatch), jnp.float32)
    rhs, bound = lax.fori_loop(0, count, first_step, (zero_rhs, zero_bound))
    rhs_all, bound_all = lax.psum((rhs, bound), ("pix", "rep"))
    slip_all = rhs_all / bound_all
    sweep_slip_half = slip_all.astype(jnp.bfloat16)

    def sweep_step(index, rhs_now):
        tile, start = tile_at(index)
        guess = lax.dot_general(
            sweep_slip_half, tile, (((1,), (1,)), ((), ())), preferred_element_type=jnp.float32
        )
        resid = (lax.dynamic_slice_in_dim(series, start, width, 1) - guess).astype(jnp.bfloat16)
        return rhs_now + jnp.dot(resid, tile, preferred_element_type=jnp.float32)

    rhs = lax.fori_loop(0, count, sweep_step, zero_rhs)
    slip_all = slip_all + lax.psum(rhs, ("pix", "rep")) / bound_all
    slip_half = slip_all.astype(jnp.bfloat16)
    slip_own = lax.dynamic_slice_in_dim(slip_all, lax.axis_index(("pix", "rep")) * own, own, 1)

    def final_step(index, predicted):
        tile, start = tile_at(index)
        block = lax.dot_general(
            slip_half, tile, (((1,), (1,)), ((), ())), preferred_element_type=jnp.float32
        )
        return lax.dynamic_update_slice_in_dim(predicted, block, start, 1)

    predicted = lax.fori_loop(0, count, final_step, jnp.zeros((epochs_count, pix_dev), jnp.float32))
    return (predicted, slip_own)


def solution(mesh):
    placed = (P(("pix", "rep"), None), P(), P(None, ("pix", "rep")), P(), P())
    return jax.shard_map(
        on_device,
        mesh=mesh,
        in_specs=placed,
        out_specs=(P(None, ("pix", "rep")), P(None, ("pix", "rep"))),
        check_vma=False,
    )
```

profile of v0, /device:TPU:0, one launch (start us, length us, event | category | flops | bytes accessed | tf_op | source)
XLA Modules:
  0.0 731.8 jit_solution(1607313868562399574)
XLA Ops:
  7.2 7.5 %all-to-all-start = ((f32[8,32,4096]{2,0,1:T(8,128)}), f32[8,32,4096]{2,0,1:T(8,128)}, u32[]{:S(2)}, u32[]{:S(2)}) async-start(f32[8,32,4096]{2,0,1:T(8,128)} %bitcast.110), calls=%async_computation | async-start | bytes 8388608 | tf_op jit(solution)/shard_map/all_to_all | solution.py:58
  15.4 5.8 cholesky.16
  22.6 4.9 custom-call.10
  28.2 80.2 %all-to-all-done = f32[8,32,4096]{2,0,1:T(8,128)} async-done(((f32[8,32,4096]{2,0,1:T(8,128)}), f32[8,32,4096]{2,0,1:T(8,128)}, u32[]{:S(2)}, u32[]{:S(2)}) %all-to-all-start) | async-done | bytes 4194336 | tf_op jit(solution)/shard_map/all_to_all | solution.py:58
  108.4 5.8 fusion.93
  114.1 168.4 %while.53 = (s32[]{:T(128)}, f32[64,4096]{1,0:T(8,128)S(1)}, f32[1,4096]{1,0:T(1,128)S(1)}, bf16[64,4096]{1,0:T(8,128)(2,1)S(1)}, f32[1,4096]{1,0:T(1,128)S(1)},...) while((s32[]{:T(128)}, f32[64,4096]{1,0:T(8,128)S(1)}, ...), condition=%wide.region_4.5_spmd.clone, body=%wide.region_2.4_spmd.clone.sunk | while | flops 373867008 | bytes 2590974 | solution.py:84
  114.3 0.9 constant_dynamic-slice_fusion.8
  115.3 6.6 convolution_add_fusion.6
  121.9 6.8 abs_reduce_fusion.2
  128.7 6.5 convolution_add_fusion.7
  136.3 6.6 convolution_add_fusion.6
  142.8 6.8 abs_reduce_fusion.2
  149.7 6.5 convolution_add_fusion.7
  157.3 6.6 convolution_add_fusion.6
  163.8 6.8 abs_reduce_fusion.2
  170.7 6.5 convolution_add_fusion.7
  178.2 6.6 convolution_add_fusion.6
  184.8 6.8 abs_reduce_fusion.2
  191.7 6.5 convolution_add_fusion.7
  199.2 6.6 convolution_add_fusion.6
  205.8 6.8 abs_reduce_fusion.2
  212.6 6.5 convolution_add_fusion.7
  220.2 6.6 convolution_add_fusion.6
  226.8 6.8 abs_reduce_fusion.2
  233.6 6.5 convolution_add_fusion.7
  241.2 6.6 convolution_add_fusion.6
  247.7 6.8 abs_reduce_fusion.2
  254.6 6.5 convolution_add_fusion.7
  262.1 6.6 convolution_add_fusion.6
  268.7 6.8 abs_reduce_fusion.2
  275.6 6.5 convolution_add_fusion.7
  282.5 1.0 copy-done.1
  283.6 38.4 %psum.22 = f32[4096]{0:T(1024)S(1)} all-reduce(f32[4096]{0:T(1024)S(1)} %bitcast.147), channel_id=1, replica_groups=mesh['pix'=8,'rep'=4] {'pix','rep'}, use_global_device_ids=true, to_apply=%region_6.7 | all-reduce | flops 4096 | bytes 32768 | tf_op jit(solution)/shard_map/psum | solution.py:85
  322.0 92.1 %all-reduce.3.cloned.1.call-done = f32[64,4096]{1,0:T(8,128)} async-done(((f32[64,4096]{1,0:T(8,128)}), f32[64,4096]{1,0:T(8,128)}) %all-reduce.3.cloned.1.call-update) | async-done | bytes 1048592 | tf_op jit(solution)/shard_map/psum | solution.py:85
  414.1 1.3 fusion.78
  415.4 117.2 %while.54 = (s32[]{:T(128)}, f32[64,4096]{1,0:T(8,128)S(1)}, f32[64,4096]{1,0:T(8,128)}, f32[1,4096]{1,0:T(1,128)S(1)}, f32[3,4096]{1,0:T(4,128)}, /*index=5*/s3...) while((s32[]{:T(128)}, f32[64,4096]{1,0:T(8,128)S(1)}, ...), condition=%wide.region_8.9_spmd.clone, body=%wide.region_7.8_spmd.clone.sunk | while | flops 600417280 | bytes 3068157 | solution.py:97
  415.4 0.9 constant_dynamic-slice_fusion.9
  416.4 13.6 %convolution_add_fusion.8 = f32[64,4096]{1,0:T(8,128)S(1)} fusion(f32[4096]{0:T(1024)S(1)} %mul.1511, f32[512]{0:T(512)S(1)} %bitcast.143, f32[4096]{0:T(1024)S(1)} %bitcast.128, f32[512]{0:T(512)S(1)} %get-tuple-element.1055, f32[512]{0:T(512)S(1)} %bitcast.142, f32[4096]{0:T(1024)S(1)} %bitcast.129, f32[512]{0:T(512)S(1)} %get-tuple-element.1058, ...), kind=kOutput, calls=%fused_computation.86.clone.1 | convolution fusion | flops 600375296 | bytes 2904069 | tf_op jit(solution)/shard_map/while/body/eval_jaxpr/dot_general | solution.py:95
  430.0 0.9 constant_dynamic-slice_fusion.9
  431.0 13.6 %convolution_add_fusion.8 = f32[64,4096]{1,0:T(8,128)S(1)} fusion(f32[4096]{0:T(1024)S(1)} %mul.1511, f32[512]{0:T(512)S(1)} %bitcast.143, f32[4096]{0:T(1024)S(1)} %bitcast.128, f32[512]{0:T(512)S(1)} %get-tuple-element.1055, f32[512]{0:T(512)S(1)} %bitcast.142, f32[4096]{0:T(1024)S(1)} %bitcast.129, f32[512]{0:T(512)S(1)} %get-tuple-element.1058, ...), kind=kOutput, calls=%fused_computation.86.clone.1 | convolution fusion | flops 600375296 | bytes 2904069 | tf_op jit(solution)/shard_map/while/body/eval_jaxpr/dot_general | solution.py:95
  444.6 0.9 constant_dynamic-slice_fusion.9
  445.6 13.6 %convolution_add_fusion.8 = f32[64,4096]{1,0:T(8,128)S(1)} fusion(f32[4096]{0:T(1024)S(1)} %mul.1511, f32[512]{0:T(512)S(1)} %bitcast.143, f32[4096]{0:T(1024)S(1)} %bitcast.128, f32[512]{0:T(512)S(1)} %get-tuple-element.1055, f32[512]{0:T(512)S(1)} %bitcast.142, f32[4096]{0:T(1024)S(1)} %bitcast.129, f32[512]{0:T(512)S(1)} %get-tuple-element.1058, ...), kind=kOutput, calls=%fused_computation.86.clone.1 | convolution fusion | flops 600375296 | bytes 2904069 | tf_op jit(solution)/shard_map/while/body/eval_jaxpr/dot_general | solution.py:95
  459.3 0.9 constant_dynamic-slice_fusion.9
  460.3 13.6 %convolution_add_fusion.8 = f32[64,4096]{1,0:T(8,128)S(1)} fusion(f32[4096]{0:T(1024)S(1)} %mul.1511, f32[512]{0:T(512)S(1)} %bitcast.143, f32[4096]{0:T(1024)S(1)} %bitcast.128, f32[512]{0:T(512)S(1)} %get-tuple-element.1055, f32[512]{0:T(512)S(1)} %bitcast.142, f32[4096]{0:T(1024)S(1)} %bitcast.129, f32[512]{0:T(512)S(1)} %get-tuple-element.1058, ...), kind=kOutput, calls=%fused_computation.86.clone.1 | convolution fusion | flops 600375296 | bytes 2904069 | tf_op jit(solution)/shard_map/while/body/eval_jaxpr/dot_general | solution.py:95
  474.9 13.6 %convolution_add_fusion.8 = f32[64,4096]{1,0:T(8,128)S(1)} fusion(f32[4096]{0:T(1024)S(1)} %mul.1511, f32[512]{0:T(512)S(1)} %bitcast.143, f32[4096]{0:T(1024)S(1)} %bitcast.128, f32[512]{0:T(512)S(1)} %get-tuple-element.1055, f32[512]{0:T(512)S(1)} %bitcast.142, f32[4096]{0:T(1024)S(1)} %bitcast.129, f32[512]{0:T(512)S(1)} %get-tuple-element.1058, ...), kind=kOutput, calls=%fused_computation.86.clone.1 | convolution fusion | flops 600375296 | bytes 2904069 | tf_op jit(solution)/shard_map/while/body/eval_jaxpr/dot_general | solution.py:95
  488.5 0.9 constant_dynamic-slice_fusion.9
  489.5 13.6 %convolution_add_fusion.8 = f32[64,4096]{1,0:T(8,128)S(1)} fusion(f32[4096]{0:T(1024)S(1)} %mul.1511, f32[512]{0:T(512)S(1)} %bitcast.143, f32[4096]{0:T(1024)S(1)} %bitcast.128, f32[512]{0:T(512)S(1)} %get-tuple-element.1055, f32[512]{0:T(512)S(1)} %bitcast.142, f32[4096]{0:T(1024)S(1)} %bitcast.129, f32[512]{0:T(512)S(1)} %get-tuple-element.1058, ...), kind=kOutput, calls=%fused_computation.86.clone.1 | convolution fusion | flops 600375296 | bytes 2904069 | tf_op jit(solution)/shard_map/while/body/eval_jaxpr/dot_general | solution.py:95
  504.1 13.6 %convolution_add_fusion.8 = f32[64,4096]{1,0:T(8,128)S(1)} fusion(f32[4096]{0:T(1024)S(1)} %mul.1511, f32[512]{0:T(512)S(1)} %bitcast.143, f32[4096]{0:T(1024)S(1)} %bitcast.128, f32[512]{0:T(512)S(1)} %get-tuple-element.1055, f32[512]{0:T(512)S(1)} %bitcast.142, f32[4096]{0:T(1024)S(1)} %bitcast.129, f32[512]{0:T(512)S(1)} %get-tuple-element.1058, ...), kind=kOutput, calls=%fused_computation.86.clone.1 | convolution fusion | flops 600375296 | bytes 2904069 | tf_op jit(solution)/shard_map/while/body/eval_jaxpr/dot_general | solution.py:95
  518.8 13.6 %convolution_add_fusion.8 = f32[64,4096]{1,0:T(8,128)S(1)} fusion(f32[4096]{0:T(1024)S(1)} %mul.1511, f32[512]{0:T(512)S(1)} %bitcast.143, f32[4096]{0:T(1024)S(1)} %bitcast.128, f32[512]{0:T(512)S(1)} %get-tuple-element.1055, f32[512]{0:T(512)S(1)} %bitcast.142, f32[4096]{0:T(1024)S(1)} %bitcast.129, f32[512]{0:T(512)S(1)} %get-tuple-element.1058, ...), kind=kOutput, calls=%fused_computation.86.clone.1 | convolution fusion | flops 600375296 | bytes 2904069 | tf_op jit(solution)/shard_map/while/body/eval_jaxpr/dot_general | solution.py:95
  532.5 1.0 copy-done.2
  533.5 129.8 %all-reduce.5.cloned.1.call-done = f32[64,4096]{1,0:T(8,128)} async-done(((f32[64,4096]{1,0:T(8,128)}), f32[64,4096]{1,0:T(8,128)}) %all-reduce.5.cloned.1.call-update) | async-done | bytes 1048592 | tf_op jit(solution)/shard_map/psum | solution.py:98
  663.3 1.4 fusion.91
  664.8 59.0 %while.52 = (s32[]{:T(128)}, f32[64,4096]{1,0:T(8,128)S(1)}, f32[1,4096]{1,0:T(1,128)S(1)}, f32[3,4096]{1,0:T(4,128)}, s32[]{:T(128)}, /*index=5*/f32[1,4096]{1,...) while((s32[]{:T(128)}, f32[64,4096]{1,0:T(8,128)S(1)}, ...), condition=%wide.region_11.12_spmd, body=%wide.region_10.11_spmd.sunk | while | flops 299934720 | bytes 895211 | solution.py:109
  665.8 6.3 fusion.114
  672.2 0.9 constant_dynamic-slice_fusion.7
  673.2 6.4 fusion.114
  680.6 6.4 fusion.114
  687.9 6.3 fusion.114
  694.3 0.9 constant_dynamic-slice_fusion.7
  695.3 6.4 fusion.114
  701.7 0.9 constant_dynamic-slice_fusion.7
  702.7 6.4 fusion.114
  710.1 6.3 fusion.114
  717.5 6.4 fusion.114
  (153 shorter events, 19.2 us)
Async XLA Ops:
  7.2 7.6 %copy-start.7 = (s32[2,256]{1,0:T(2,128)S(1)}, s32[2,256]{1,0:T(2,128)}, u32[]{:S(2)}) copy-start(s32[2,256]{1,0:T(2,128)} %param.12) | copy-start | bytes 6148
  7.2 20.3 %copy-start.6 = (s32[4096]{0:T(1024)S(1)}, s32[4096]{0:T(1024)}, u32[]{:S(2)}) copy-start(s32[4096]{0:T(1024)} %param.15) | copy-start | bytes 49156
  7.2 20.9 %copy-start.5 = (s32[2,4096]{1,0:T(2,128)S(1)}, s32[2,4096]{1,0:T(2,128)}, u32[]{:S(2)}) copy-start(s32[2,4096]{1,0:T(2,128)} %param.14) | copy-start | bytes 98308
  7.2 101.2 %all-to-all-start = ((f32[8,32,4096]{2,0,1:T(8,128)}), f32[8,32,4096]{2,0,1:T(8,128)}, u32[]{:S(2)}, u32[]{:S(2)}) async-start(f32[8,32,4096]{2,0,1:T(8,128)} %bitcast.110), calls=%async_computation | async-start | bytes 8388608 | tf_op jit(solution)/shard_map/all_to_all | solution.py:58
  14.7 399.4 %all-reduce.3.cloned.1.call-start = ((), (), s32[]{:S(2)}) async-start(), calls=%async_computation.1 | async-start | bytes 2097152 | tf_op jit(solution)/shard_map/psum | solution.py:85
  282.5 1.0 copy-start.1
  283.5 379.8 %all-reduce.5.cloned.1.call-start = ((), (), s32[]{:S(2)}) async-start(), calls=%async_computation.2 | async-start | bytes 2097152 | tf_op jit(solution)/shard_map/psum | solution.py:98
  322.0 93.4 %copy-start.4 = (f32[4096]{0:T(1024)}, f32[4096]{0:T(1024)S(1)}, u32[]{:S(2)}) copy-start(f32[4096]{0:T(1024)S(1)} %psum.22) | copy-start | bytes 49156
  415.4 248.0 %copy-start = (f32[64,4096]{1,0:T(8,128)S(1)}, f32[64,4096]{1,0:T(8,128)}, u32[]{:S(2)}) copy-start(f32[64,4096]{1,0:T(8,128)} %all-reduce.3.cloned.1.call-done) | copy-start | bytes 3145732
  532.5 1.0 copy-start.2
  723.8 1.0 copy-start.3
Sparse Core Ops, SparseCore 0:
  283.7 130.3 all-reduce.2
  533.7 129.6 all-reduce.4
where the time goes:
time: 738 us; the launch traced here: 732 us
  waiting for transfers between devices  302 us (41%)
  matrix products  271 us (37%)
  other arithmetic  71.6 us (10%)
  blocking collectives  38.4 us (5%)
  local copies, waits for them, and re-layouts  24.6 us (3%)
  between operations  14.5 us (2%)
  starting transfers between devices  7.54 us (1%)
    psum x1, waiting for transfers between devices, on_device(): slip_all = slip_all + lax.psum(rhs, ('pix', 'rep')) / bound_all  130 us
    dot_general x8, matrix products, sweep_step(): return rhs_now + jnp.dot(resid, tile, preferred_element_type=jnp.float32)  109 us
    psum x1, waiting for transfers between devices, on_device(): rhs_all, bound_all = lax.psum((rhs, bound), ('pix', 'rep'))  92.1 us
    all_to_all x1, waiting for transfers between devices, on_device(): lax.all_to_all(pieces, ('pix', 'rep'), split_axis=1, concat_axis=0, tiled...  80.2 us
    reduce_sum x8, other arithmetic, first_step(): weight = jnp.sum(magnitude.astype(jnp.float32), axis=1).astype(jnp.bfloat16)  54.8 us
    dot_general x8, matrix products, first_step(): rhs = rhs + jnp.dot(resid, tile, preferred_element_type=jnp.float32)  52.5 us
    dot_general x8, matrix products, first_step(): jnp.dot(weight[None, :], magnitude, preferred_element_type=jnp.float32)  52.4 us
    dot_general x8, matrix products, final_step(): lax.dot_general(slip_half, tile, (((1,), (1,)), ((), ())), preferred_elem...  50.8 us
  transfers between devices with their start and end apart: 3, of which 3 were waited for; matrix products, arithmetic and copies ran while one was open for 2% of the time, Pallas kernels for 0%

commit v1 on v0

--- a/solution.py
+++ b/solution.py
@@ -2,6 +2,7 @@
 import jax.numpy as jnp
 from jax import lax
 from jax.sharding import PartitionSpec as P
+from jax.lax import all_to_all, axis_size
 
 NEP = 64
 IMG_W = 1024
@@ -10,6 +11,19 @@
 damping = 0.5
 depth_base = 0.5
 depth_step = 0.25
+
+
+def render_the_case(obj):
+    kept_arr = jnp.concatenate(
+        all_to_all(
+            jnp.stack(jnp.split(obj, axis_size(("pix", "rep")), axis=1)),
+            axis_name=("pix", "rep"),
+            split_axis=0,
+            concat_axis=0,
+        ),
+        axis=0,
+    )
+    return kept_arr
 
 
 def sbas_inverse(epoch_pairs, epochs_count):
@@ -55,7 +69,7 @@
     pieces = interferograms.reshape(ifg_dev, devices, pix_dev)
     series = jnp.dot(
         pseudo,
-        lax.all_to_all(pieces, ("pix", "rep"), split_axis=1, concat_axis=0, tiled=True)[:, 0, :],
+        render_the_case(pieces)[:, 0, :],
         precision=lax.Precision.HIGHEST,
         preferred_element_type=jnp.float32,
     )

time: 738 us -> 774 us (1.049)
  local copies, waits for them, and re-layouts: 24.6 us -> 60.5 us
    unnamed x16 -> x51, local copies, waits for them, and re-layouts: 2.28 us -> 37.5 us
where the time goes in v1:
time: 774 us; the launch traced here: 768 us
  waiting for transfers between devices  302 us (39%)
  matrix products  271 us (35%)
  other arithmetic  71.6 us (9%)
  local copies, waits for them, and re-layouts  60.5 us (8%)
  blocking collectives  38.4 us (5%)
  between operations  14.5 us (2%)
    psum x1, waiting for transfers between devices, on_device(): slip_all = slip_all + lax.psum(rhs, ('pix', 'rep')) / bound_all  130 us
    dot_general x8, matrix products, sweep_step(): return rhs_now + jnp.dot(resid, tile, preferred_element_type=jnp.float32)  109 us
    psum x1, waiting for transfers between devices, on_device(): rhs_all, bound_all = lax.psum((rhs, bound), ('pix', 'rep'))  92 us
    all_to_all x1, waiting for transfers between devices, render_the_case(): all_to_all(jnp.stack(jnp.split(obj, axis_size(('pix', 'rep')), axis=1)),...  80.2 us
    reduce_sum x8, other arithmetic, first_step(): weight = jnp.sum(magnitude.astype(jnp.float32), axis=1).astype(jnp.bfloat16)  54.8 us
    dot_general x8, matrix products, first_step(): rhs = rhs + jnp.dot(resid, tile, preferred_element_type=jnp.float32)  52.5 us
    dot_general x8, matrix products, first_step(): jnp.dot(weight[None, :], magnitude, preferred_element_type=jnp.float32)  52.4 us
    dot_general x8, matrix products, final_step(): lax.dot_general(slip_half, tile, (((1,), (1,)), ((), ())), preferred_elem...  50.8 us
  transfers between devices with their start and end apart: 3, of which 3 were waited for; matrix products, arithmetic and copies ran while one was open for 2% of the time, Pallas kernels for 0%

profile of v1, /device:TPU:0, one launch (start us, length us, event | category | flops | bytes accessed | tf_op | source)
XLA Modules:
  0.0 767.8 jit_solution(6884635113125099276)
XLA Ops:
  7.2 1.7 fusion.110
  8.9 1.6 fusion.109
  10.5 1.6 fusion.108
  12.0 1.6 fusion.107
  15.2 1.6 fusion.105
  18.3 1.6 fusion.103
  19.9 1.6 fusion.102
  21.5 1.6 fusion.101
  23.0 1.6 fusion.100
  24.6 1.6 fusion.99
  26.2 1.6 fusion.98
  29.3 1.6 fusion.96
  30.9 1.6 fusion.95
  43.1 7.5 all-to-all-start
  51.4 5.8 cholesky.16
  58.5 4.9 custom-call.10
  64.1 80.2 %all-to-all-done = f32[32,8,1,4096]{3,1,2,0:T(8,128)} async-done(((f32[32,8,1,4096]{3,1,2,0:T(8,128)}), f32[32,8,1,4096]{3,1,2,0:T(8,128)}, u32[]{:S(2)}, u32[]{:S(2)}) %all-to-all-start) | async-done | bytes 4194336 | tf_op jit(solution)/shard_map/all_to_all | solution.py:18
  144.3 5.8 fusion.125
  150.1 168.4 %while.53 = (s32[]{:T(128)}, f32[64,4096]{1,0:T(8,128)S(1)}, f32[1,4096]{1,0:T(1,128)S(1)}, bf16[64,4096]{1,0:T(8,128)(2,1)S(1)}, f32[1,4096]{1,0:T(1,128)S(1)},...) while((s32[]{:T(128)}, f32[64,4096]{1,0:T(8,128)S(1)}, ...), condition=%wide.region_4.5_spmd.clone, body=%wide.region_2.4_spmd.clone.sunk | while | flops 373867008 | bytes 2590974 | solution.py:98
  151.2 6.6 convolution_add_fusion.6
  157.8 6.8 abs_reduce_fusion.2
  164.7 6.5 convolution_add_fusion.7
  172.2 6.6 convolution_add_fusion.6
  178.8 6.8 abs_reduce_fusion.2
  185.6 6.5 convolution_add_fusion.7
  193.2 6.6 convolution_add_fusion.6
  199.8 6.8 abs_reduce_fusion.2
  206.6 6.5 convolution_add_fusion.7
  214.2 6.6 convolution_add_fusion.6
  220.7 6.8 abs_reduce_fusion.2
  227.6 6.5 convolution_add_fusion.7
  235.2 6.6 convolution_add_fusion.6
  241.7 6.8 abs_reduce_fusion.2
  248.6 6.5 convolution_add_fusion.7
  256.1 6.6 convolution_add_fusion.6
  262.7 6.8 abs_reduce_fusion.2
  269.6 6.5 convolution_add_fusion.7
  277.1 6.6 convolution_add_fusion.6
  283.7 6.8 abs_reduce_fusion.2
  290.5 6.5 convolution_add_fusion.7
  298.1 6.6 convolution_add_fusion.6
  304.6 6.8 abs_reduce_fusion.2
  311.5 6.5 convolution_add_fusion.7
  319.5 38.4 %psum.22 = f32[4096]{0:T(1024)S(1)} all-reduce(f32[4096]{0:T(1024)S(1)} %bitcast.302), channel_id=1, replica_groups=mesh['pix'=8,'rep'=4] {'pix','rep'}, use_global_device_ids=true, to_apply=%region_6.7 | all-reduce | flops 4096 | bytes 32768 | tf_op jit(solution)/shard_map/psum | solution.py:99
  357.9 92.0 %all-reduce.3.cloned.1.call-done = f32[64,4096]{1,0:T(8,128)} async-done(((f32[64,4096]{1,0:T(8,128)}), f32[64,4096]{1,0:T(8,128)}) %all-reduce.3.cloned.1.call-update) | async-done | bytes 1048592 | tf_op jit(solution)/shard_map/psum | solution.py:99
  451.3 117.2 %while.54 = (s32[]{:T(128)}, f32[64,4096]{1,0:T(8,128)S(1)}, f32[64,4096]{1,0:T(8,128)}, f32[1,4096]{1,0:T(1,128)S(1)}, f32[3,4096]{1,0:T(4,128)}, /*index=5*/s3...) while((s32[]{:T(128)}, f32[64,4096]{1,0:T(8,128)S(1)}, ...), condition=%wide.region_8.9_spmd.clone, body=%wide.region_7.8_spmd.clone.sunk | while | flops 600417280 | bytes 3068157 | solution.py:111
  452.3 13.6 %convolution_add_fusion.8 = f32[64,4096]{1,0:T(8,128)S(1)} fusion(f32[4096]{0:T(1024)S(1)} %mul.1511, f32[512]{0:T(512)S(1)} %bitcast.298, f32[4096]{0:T(1024)S(1)} %bitcast.283, f32[512]{0:T(512)S(1)} %get-tuple-element.1055, f32[512]{0:T(512)S(1)} %bitcast.297, f32[4096]{0:T(1024)S(1)} %bitcast.284, f32[512]{0:T(512)S(1)} %get-tuple-element.1058, ...), kind=kOutput, calls=%fused_computation.86.clone.1 | convolution fusion | flops 600375296 | bytes 2904069 | tf_op jit(solution)/shard_map/while/body/eval_jaxpr/dot_general | solution.py:109
  466.9 13.6 %convolution_add_fusion.8 = f32[64,4096]{1,0:T(8,128)S(1)} fusion(f32[4096]{0:T(1024)S(1)} %mul.1511, f32[512]{0:T(512)S(1)} %bitcast.298, f32[4096]{0:T(1024)S(1)} %bitcast.283, f32[512]{0:T(512)S(1)} %get-tuple-element.1055, f32[512]{0:T(512)S(1)} %bitcast.297, f32[4096]{0:T(1024)S(1)} %bitcast.284, f32[512]{0:T(512)S(1)} %get-tuple-element.1058, ...), kind=kOutput, calls=%fused_computation.86.clone.1 | convolution fusion | flops 600375296 | bytes 2904069 | tf_op jit(solution)/shard_map/while/body/eval_jaxpr/dot_general | solution.py:109
  481.5 13.6 %convolution_add_fusion.8 = f32[64,4096]{1,0:T(8,128)S(1)} fusion(f32[4096]{0:T(1024)S(1)} %mul.1511, f32[512]{0:T(512)S(1)} %bitcast.298, f32[4096]{0:T(1024)S(1)} %bitcast.283, f32[512]{0:T(512)S(1)} %get-tuple-element.1055, f32[512]{0:T(512)S(1)} %bitcast.297, f32[4096]{0:T(1024)S(1)} %bitcast.284, f32[512]{0:T(512)S(1)} %get-tuple-element.1058, ...), kind=kOutput, calls=%fused_computation.86.clone.1 | convolution fusion | flops 600375296 | bytes 2904069 | tf_op jit(solution)/shard_map/while/body/eval_jaxpr/dot_general | solution.py:109
  496.2 13.6 %convolution_add_fusion.8 = f32[64,4096]{1,0:T(8,128)S(1)} fusion(f32[4096]{0:T(1024)S(1)} %mul.1511, f32[512]{0:T(512)S(1)} %bitcast.298, f32[4096]{0:T(1024)S(1)} %bitcast.283, f32[512]{0:T(512)S(1)} %get-tuple-element.1055, f32[512]{0:T(512)S(1)} %bitcast.297, f32[4096]{0:T(1024)S(1)} %bitcast.284, f32[512]{0:T(512)S(1)} %get-tuple-element.1058, ...), kind=kOutput, calls=%fused_computation.86.clone.1 | convolution fusion | flops 600375296 | bytes 2904069 | tf_op jit(solution)/shard_map/while/body/eval_jaxpr/dot_general | solution.py:109
  510.8 13.6 %convolution_add_fusion.8 = f32[64,4096]{1,0:T(8,128)S(1)} fusion(f32[4096]{0:T(1024)S(1)} %mul.1511, f32[512]{0:T(512)S(1)} %bitcast.298, f32[4096]{0:T(1024)S(1)} %bitcast.283, f32[512]{0:T(512)S(1)} %get-tuple-element.1055, f32[512]{0:T(512)S(1)} %bitcast.297, f32[4096]{0:T(1024)S(1)} %bitcast.284, f32[512]{0:T(512)S(1)} %get-tuple-element.1058, ...), kind=kOutput, calls=%fused_computation.86.clone.1 | convolution fusion | flops 600375296 | bytes 2904069 | tf_op jit(solution)/shard_map/while/body/eval_jaxpr/dot_general | solution.py:109
  525.4 13.6 %convolution_add_fusion.8 = f32[64,4096]{1,0:T(8,128)S(1)} fusion(f32[4096]{0:T(1024)S(1)} %mul.1511, f32[512]{0:T(512)S(1)} %bitcast.298, f32[4096]{0:T(1024)S(1)} %bitcast.283, f32[512]{0:T(512)S(1)} %get-tuple-element.1055, f32[512]{0:T(512)S(1)} %bitcast.297, f32[4096]{0:T(1024)S(1)} %bitcast.284, f32[512]{0:T(512)S(1)} %get-tuple-element.1058, ...), kind=kOutput, calls=%fused_computation.86.clone.1 | convolution fusion | flops 600375296 | bytes 2904069 | tf_op jit(solution)/shard_map/while/body/eval_jaxpr/dot_general | solution.py:109
  540.0 13.6 %convolution_add_fusion.8 = f32[64,4096]{1,0:T(8,128)S(1)} fusion(f32[4096]{0:T(1024)S(1)} %mul.1511, f32[512]{0:T(512)S(1)} %bitcast.298, f32[4096]{0:T(1024)S(1)} %bitcast.283, f32[512]{0:T(512)S(1)} %get-tuple-element.1055, f32[512]{0:T(512)S(1)} %bitcast.297, f32[4096]{0:T(1024)S(1)} %bitcast.284, f32[512]{0:T(512)S(1)} %get-tuple-element.1058, ...), kind=kOutput, calls=%fused_computation.86.clone.1 | convolution fusion | flops 600375296 | bytes 2904069 | tf_op jit(solution)/shard_map/while/body/eval_jaxpr/dot_general | solution.py:109
  554.7 13.6 %convolution_add_fusion.8 = f32[64,4096]{1,0:T(8,128)S(1)} fusion(f32[4096]{0:T(1024)S(1)} %mul.1511, f32[512]{0:T(512)S(1)} %bitcast.298, f32[4096]{0:T(1024)S(1)} %bitcast.283, f32[512]{0:T(512)S(1)} %get-tuple-element.1055, f32[512]{0:T(512)S(1)} %bitcast.297, f32[4096]{0:T(1024)S(1)} %bitcast.284, f32[512]{0:T(512)S(1)} %get-tuple-element.1058, ...), kind=kOutput, calls=%fused_computation.86.clone.1 | convolution fusion | flops 600375296 | bytes 2904069 | tf_op jit(solution)/shard_map/while/body/eval_jaxpr/dot_general | solution.py:109
  569.4 129.8 %all-reduce.5.cloned.1.call-done = f32[64,4096]{1,0:T(8,128)} async-done(((f32[64,4096]{1,0:T(8,128)}), f32[64,4096]{1,0:T(8,128)}) %all-reduce.5.cloned.1.call-update) | async-done | bytes 1048592 | tf_op jit(solution)/shard_map/psum | solution.py:112
  700.7 59.0 %while.52 = (s32[]{:T(128)}, f32[64,4096]{1,0:T(8,128)S(1)}, f32[1,4096]{1,0:T(1,128)S(1)}, f32[3,4096]{1,0:T(4,128)}, s32[]{:T(128)}, /*index=5*/f32[1,4096]{1,...) while((s32[]{:T(128)}, f32[64,4096]{1,0:T(8,128)S(1)}, ...), condition=%wide.region_11.12_spmd, body=%wide.region_10.11_spmd.sunk | while | flops 299934720 | bytes 895211 | solution.py:123
  701.7 6.4 fusion.146
  709.1 6.4 fusion.146
  716.5 6.3 fusion.146
  723.9 6.4 fusion.146
  731.2 6.4 fusion.146
  738.6 6.3 fusion.146
  746.0 6.3 fusion.146
  753.4 6.4 fusion.146
  (189 shorter events, 47.2 us)
Async XLA Ops:
  7.2 25.3 %copy-start = (f32[8,131072]{1,0:T(8,128)S(1)}, f32[8,131072]{1,0:T(8,128)}, u32[]{:S(2)}) copy-start(f32[8,131072]{1,0:T(8,128)} %param.11) | copy-start | bytes 12582916
  43.1 7.5 copy-start.9
  43.1 20.3 %copy-start.8 = (s32[4096]{0:T(1024)S(1)}, s32[4096]{0:T(1024)}, u32[]{:S(2)}) copy-start(s32[4096]{0:T(1024)} %param.15) | copy-start | bytes 49156
  43.1 20.9 %copy-start.7 = (s32[2,4096]{1,0:T(2,128)S(1)}, s32[2,4096]{1,0:T(2,128)}, u32[]{:S(2)}) copy-start(s32[2,4096]{1,0:T(2,128)} %param.14) | copy-start | bytes 98308
  43.1 101.2 %all-to-all-start = ((f32[32,8,1,4096]{3,1,2,0:T(8,128)}), f32[32,8,1,4096]{3,1,2,0:T(8,128)}, u32[]{:S(2)}, u32[]{:S(2)}) async-start(f32[32,8,1,4096]{3,1,2,0:T(8,128)} %fusion.79), calls=%async_computation | async-start | bytes 8388608 | tf_op jit(solution)/shard_map/all_to_all | solution.py:18
  50.6 399.3 %all-reduce.3.cloned.1.call-start = ((), (), s32[]{:S(2)}) async-start(), calls=%async_computation.1 | async-start | bytes 2097152 | tf_op jit(solution)/shard_map/psum | solution.py:99
  318.4 1.0 copy-start.2
  319.5 379.8 %all-reduce.5.cloned.1.call-start = ((), (), s32[]{:S(2)}) async-start(), calls=%async_computation.2 | async-start | bytes 2097152 | tf_op jit(solution)/shard_map/psum | solution.py:112
  357.9 93.3 %copy-start.5 = (f32[4096]{0:T(1024)}, f32[4096]{0:T(1024)S(1)}, u32[]{:S(2)}) copy-start(f32[4096]{0:T(1024)S(1)} %psum.22) | copy-start | bytes 49156
  451.2 248.0 %copy-start.1 = (f32[64,4096]{1,0:T(8,128)S(1)}, f32[64,4096]{1,0:T(8,128)}, u32[]{:S(2)}) copy-start(f32[64,4096]{1,0:T(8,128)} %all-reduce.3.cloned.1.call-done) | copy-start | bytes 3145732
  451.2 248.0 %copy-start.6 = (f32[4096]{0:T(1024)S(1)}, f32[4096]{0:T(1024)}, u32[]{:S(2)}) copy-start(f32[4096]{0:T(1024)} %copy-done.5) | copy-start | bytes 49156
  568.4 1.0 copy-start.3
  759.8 1.0 copy-start.4
Sparse Core Ops, SparseCore 0:
  319.6 130.2 all-reduce.2
  569.6 129.6 all-reduce.4
